TPU v7x, 32 devices: a whole 2x2x4 slice. The times are simulated.
32 devices in a mesh: ctx: 4 (over z), head: 8 (over y, x, core).
Axes of the slice: x: 2, y: 2, z: 4, core: 2. Of those that a mesh axis runs over, the one named last changes fastest.
Arguments:
- video: bfloat16 [3072, 4096], P('ctx', 'head'), may hold values from -6 to 6
- audio: bfloat16 [384, 2048], P('ctx', 'head'), may hold values from -6 to 6
- video_gain: float32 [4096], P('head'), may hold values from 0.1 to 1.9
- audio_gain: float32 [2048], P('head'), may hold values from 0.1 to 1.9
- video_qkv: bfloat16 [4096, 3, 4096], P(None, None, 'head'), as said below
- video_cross: bfloat16 [4096, 3, 2048], P(None, None, 'head'), as said below
- audio_cross: bfloat16 [2048, 3, 2048], P(None, None, 'head'), as said below
- video_out: bfloat16 [4096, 4096], P('head'), may hold values from -0.09375 to 0.09375
- cross_video_out: bfloat16 [2048, 4096], P('head'), may hold values from -0.125 to 0.125
- cross_audio_out: bfloat16 [2048, 2048], P('head'), may hold values from -0.125 to 0.125
Outputs:
- video_result: bfloat16 [3072, 4096], P('ctx', 'head')
- audio_result: bfloat16 [384, 2048], P('ctx', 'head')
Inputs may be any that keep to these rules, and one draw needn't show every extreme that they name: `video_qkv`: entries lie within -32 / sqrt(4096) and 32 / sqrt(4096). `video_cross`: entries lie within -32 / sqrt(4096) and 32 / sqrt(4096). `audio_cross`: entries lie within -32 / sqrt(2048) and 32 / sqrt(2048).
All inputs are finite; a program needn't handle non-finite values.
Results may differ from a plain program's by a relative error of at most 0.014.
The roundings to bfloat16 on the way count: a program that leaves them out, or rounds other values in their place, can miss the bound.
Values may be sent and summed in bfloat16 or wider, within the bound.
A program may use at most 128 MiB of HBM per device.

v0:
```python
import functools
import math

import jax
import jax.numpy as jnp
from jax import lax
from jax.experimental import pallas as pl
from jax.experimental.pallas import tpu as pltpu

from jax.sharding import PartitionSpec as P

HD = 128


EPSILON = 1e-06


def split_heads(matrix):
    return matrix.reshape(matrix.shape[0], -1, HD).transpose(1, 0, 2)


def join_heads(blocks):
    return blocks.transpose(1, 0, 2).reshape(blocks.shape[1], -1)


def attend(queries, keys, values):
    scale = HD ** (-0.5)

    def one_head(operands):
        query_block, key_block, value_block = operands
        scores = jnp.dot(query_block, key_block.T, preferred_element_type=jnp.float32) * scale
        highest = jnp.max(scores, axis=1, keepdims=True)
        weights = jnp.exp(scores - highest)
        totals = jnp.sum(weights, axis=1, keepdims=True)
        return (
            jnp.dot(weights.astype(jnp.bfloat16), value_block, preferred_element_type=jnp.float32)
            / totals
        )

    blocks = lax.map(one_head, (split_heads(queries), split_heads(keys), split_heads(values)))
    return join_heads(blocks).astype(jnp.bfloat16)


def plain_body(
    video,
    audio,
    video_gain,
    audio_gain,
    video_qkv,
    video_cross,
    audio_cross,
    video_out,
    cross_video_out,
    cross_audio_out,
):
    scale = HD ** (-0.5)
    video_wide = video.astype(jnp.float32)
    audio_wide = audio.astype(jnp.float32)
    video_squares, audio_squares = lax.psum(
        (jnp.sum(video_wide * video_wide, axis=1), jnp.sum(audio_wide * audio_wide, axis=1)), "head"
    )
    video_rate = lax.rsqrt(video_squares / video_qkv.shape[0] + EPSILON)
    audio_rate = lax.rsqrt(audio_squares / audio_cross.shape[0] + EPSILON)
    video_scaled = (video_wide * video_gain).astype(jnp.bfloat16)
    audio_scaled = (audio_wide * audio_gain).astype(jnp.bfloat16)
    self_weight = video_qkv.reshape(video_qkv.shape[0], -1)
    mixed_weight = video_cross.reshape(video_cross.shape[0], -1)
    audio_weight = audio_cross.reshape(audio_cross.shape[0], -1)
    self_width = video_qkv.shape[2]
    cross_width = video_cross.shape[2]
    video_rows = video.shape[0]
    segment = lax.all_gather(video_scaled, "head", axis=1, tiled=True)
    self_acc = jnp.dot(segment, self_weight, preferred_element_type=jnp.float32)
    mixed_acc = jnp.dot(segment, mixed_weight, preferred_element_type=jnp.float32)
    audio_acc = jnp.dot(
        lax.all_gather(audio_scaled, "head", axis=1, tiled=True),
        audio_weight,
        preferred_element_type=jnp.float32,
    )
    self_proj = (self_acc * video_rate[:, None]).astype(jnp.bfloat16)
    video_mixed = (mixed_acc * video_rate[:, None]).astype(jnp.bfloat16)
    audio_mixed = (audio_acc * audio_rate[:, None]).astype(jnp.bfloat16)
    query_heads = split_heads(self_proj[:, :self_width])
    local_heads = query_heads.shape[0]
    running_max = jnp.full((local_heads, video_rows), -1e30, jnp.float32)
    key_heads = split_heads(
        lax.all_gather(self_proj[:, self_width : 2 * self_width], "ctx", axis=0, tiled=True)
    )
    value_heads = split_heads(
        lax.all_gather(self_proj[:, 2 * self_width :], "ctx", axis=0, tiled=True)
    )
    scores = (
        jnp.einsum("hqd,hkd->hqk", query_heads, key_heads, preferred_element_type=jnp.float32)
        * scale
    )
    newest = jnp.maximum(running_max, jnp.max(scores, axis=2))
    weights = jnp.exp(scores - newest[:, :, None])
    running_sum = jnp.sum(weights, axis=2)
    running_acc = jnp.einsum(
        "hqk,hkd->hqd",
        weights.astype(jnp.bfloat16),
        value_heads,
        preferred_element_type=jnp.float32,
    )
    self_out = join_heads(running_acc / running_sum[:, :, None]).astype(jnp.bfloat16)
    audio_key_all, audio_value_all = (
        lax.all_gather(audio_mixed[:, cross_width : 2 * cross_width], "ctx", axis=0, tiled=True),
        lax.all_gather(audio_mixed[:, 2 * cross_width :], "ctx", axis=0, tiled=True),
    )
    video_cross_out = attend(video_mixed[:, :cross_width], audio_key_all, audio_value_all)
    queries_av = audio_mixed[:, :cross_width]
    keys_av = video_mixed[:, cross_width : 2 * cross_width]
    values_av = video_mixed[:, 2 * cross_width :]
    every_query = lax.all_gather(queries_av, "ctx", axis=0, tiled=True)
    scores = (
        jnp.einsum(
            "hqd,hkd->hqk",
            split_heads(every_query),
            split_heads(keys_av),
            preferred_element_type=jnp.float32,
        )
        * scale
    )
    highest = lax.pmax(jnp.max(scores, axis=2), "ctx")
    weights = jnp.exp(scores - highest[:, :, None])
    numerators = jnp.einsum(
        "hqk,hkd->hqd",
        weights.astype(jnp.bfloat16),
        split_heads(values_av),
        preferred_element_type=jnp.float32,
    )
    weight_totals = jnp.sum(weights, axis=2)
    own_numer, own_totals = (
        lax.psum_scatter(
            numerators.astype(jnp.bfloat16), "ctx", scatter_dimension=1, tiled=True
        ).astype(jnp.float32),
        lax.psum_scatter(
            weight_totals.astype(jnp.bfloat16), "ctx", scatter_dimension=1, tiled=True
        ).astype(jnp.float32),
    )
    audio_cross_out = join_heads(own_numer / own_totals[:, :, None]).astype(jnp.bfloat16)
    video_partial = jnp.dot(self_out, video_out, preferred_element_type=jnp.float32) + jnp.dot(
        video_cross_out, cross_video_out, preferred_element_type=jnp.float32
    )
    audio_partial = jnp.dot(audio_cross_out, cross_audio_out, preferred_element_type=jnp.float32)
    video_sum, audio_sum = (
        lax.psum_scatter(
            video_partial.astype(jnp.bfloat16), "head", scatter_dimension=1, tiled=True
        ).astype(jnp.float32),
        lax.psum_scatter(
            audio_partial.astype(jnp.bfloat16), "head", scatter_dimension=1, tiled=True
        ).astype(jnp.float32),
    )
    return (
        (video_wide + video_sum).astype(jnp.bfloat16),
        (audio_wide + audio_sum).astype(jnp.bfloat16),
    )


MESH = pl.DeviceIdType.MESH
F32 = jnp.float32
BF16 = jnp.bfloat16
VMEM_LIMIT = 62 * 1024 * 1024
CHUNK = HD
SCORE_SCALE = HD ** (-0.5) * math.log2(math.e)


def head_peer(me, flip):
    low = me % 2
    mid = (me // 2) % 2
    high = me // 4
    if flip & 1:
        low = 1 - low
    if flip & 2:
        mid = 1 - mid
    if flip & 4:
        high = 1 - high
    return high * 4 + mid * 2 + low


def remote(source, target, send, recv, device):
    return pltpu.make_async_remote_copy(
        src_ref=source,
        dst_ref=target,
        send_sem=send,
        recv_sem=recv,
        device_id=device,
        device_id_type=MESH,
    )


def diagonal(rows):
    line = lax.broadcasted_iota(jnp.int32, (rows, HD), 0)
    lane = lax.broadcasted_iota(jnp.int32, (rows, HD), 1)
    return line == lane


def to_row(column):
    rows = column.shape[0]
    spread = jnp.broadcast_to(column, (rows, HD))
    return jnp.sum(jnp.where(diagonal(rows), spread, 0.0), axis=0, keepdims=True)


def to_column(row, rows):
    spread = jnp.broadcast_to(row, (rows, HD))
    return jnp.sum(jnp.where(diagonal(rows), spread, 0.0), axis=1, keepdims=True)


def contract_last(left, right):
    return lax.dot_general(left, right, (((1,), (1,)), ((), ())), preferred_element_type=F32)


def softmax_parts(query, keys, values):
    scores = [contract_last(query, key) for key in keys]
    highest = functools.reduce(
        jnp.maximum, [jnp.max(score, axis=1, keepdims=True) for score in scores]
    )
    total = 0.0
    mixed = 0.0
    for score, value in zip(scores, values):
        weight = jnp.exp2((score - highest) * SCORE_SCALE)
        total = total + jnp.sum(weight, axis=1, keepdims=True)
        mixed = mixed + jnp.dot(weight.astype(BF16), value, preferred_element_type=F32)
    return mixed, total, highest * SCORE_SCALE


def aligned(start, size):
    return pl.ds(pl.multiple_of(start, size), size)


def entry_kernel(
    ctx_size,
    video_ref,
    audio_ref,
    video_gain_ref,
    audio_gain_ref,
    w_self_ref,
    w_cross_ref,
    w_audio_ref,
    source_ref,
    cross_out_ref,
    sound_ref,
    xs,
    xa,
    squares,
    every_square,
    w_self,
    w_cross,
    w_audio,
    heads,
    cross,
    tones,
    parts,
    parts_in,
    stats,
    stats_in,
    load,
    plane_send,
    plane_recv,
    tone_send,
    tone_recv,
    square_send,
    square_recv,
    key_send,
    key_recv,
    late_send,
    late_recv,
):
    ctx = lax.axis_index("ctx")
    me = lax.axis_index("head")
    rows, width = video_ref.shape
    audio_rows, audio_width = audio_ref.shape
    count = rows // CHUNK
    local_heads = width // HD
    cross_width = w_cross.shape[2]
    cross_heads = cross_width // HD
    peer = [head_peer(me, flip) for flip in range(8)]
    mates = [(ctx + d) % ctx_size for d in range(ctx_size)]

    plane_order = (1, 2, 0)
    loads = {}
    for i, plane in enumerate(plane_order):
        loads[plane] = pltpu.make_async_copy(w_self_ref.at[plane], w_self.at[plane], load.at[i])
        loads[plane].start()
    load_audio = pltpu.make_async_copy(w_audio_ref, w_audio, load.at[3])
    load_cross = pltpu.make_async_copy(w_cross_ref, w_cross, load.at[4])
    load_audio.start()
    load_cross.start()

    barrier = pltpu.get_barrier_semaphore()
    friends = [(ctx, peer[flip]) for flip in range(1, 8)]
    friends += [(mates[d], me) for d in range(1, ctx_size)]
    for friend in friends:
        pl.semaphore_signal(barrier, inc=1, device_id=friend, device_id_type=MESH)

    def at_rows(k):
        return aligned(k * CHUNK, CHUNK)

    def columns(block):
        return aligned(block * width, width)

    def tone_columns(block):
        return aligned(block * audio_width, audio_width)

    for k in range(count):
        wide = video_ref[pl.ds(k * CHUNK, CHUNK)].astype(F32)
        xs[pl.ds(k * CHUNK, CHUNK), columns(me)] = (wide * video_gain_ref[...]).astype(BF16)
        squares[k : k + 1] = to_row(jnp.sum(wide * wide, axis=1, keepdims=True))
    wide = audio_ref[...].astype(F32)
    xa[:, tone_columns(me)] = (wide * audio_gain_ref[...]).astype(BF16)
    squares[count : count + 1] = to_row(jnp.sum(wide * wide, axis=1, keepdims=True))
    every_square[0] = squares[...]

    pl.semaphore_wait(barrier, len(friends))

    def hop(slot, k, flip, block):
        part = xs.at[at_rows(k), columns(block)]
        return remote(part, part, plane_send.at[slot, k], plane_recv.at[slot, k], (ctx, peer[flip]))

    def tone_hop(slot, flip, block):
        part = xa.at[:, tone_columns(block)]
        return remote(part, part, tone_send.at[slot], tone_recv.at[slot], (ctx, peer[flip]))

    def direct_x(k):
        return hop(0, k, 2, me)

    def direct_y(k):
        return hop(1, k, 4, me)

    def side(k):
        return hop(2, k, 1, me)

    def far(k, parity):
        return hop(3, k, 2, peer[4]) if parity else hop(3, k, 4, peer[2])

    def side_x(k):
        return hop(4, k, 1, peer[2])

    def side_y(k):
        return hop(5, k, 1, peer[4])

    def side_far(k):
        return hop(6, k, 1, peer[6])

    tone_hops = [
        tone_hop(0, 2, me),
        tone_hop(1, 4, me),
        tone_hop(2, 1, me),
        tone_hop(3, 4, peer[2]),
        tone_hop(4, 1, peer[2]),
        tone_hop(5, 1, peer[4]),
        tone_hop(6, 1, peer[6]),
    ]
    square_hops = [
        remote(
            squares,
            every_square.at[flip],
            square_send.at[flip - 1],
            square_recv.at[flip - 1],
            (ctx, peer[flip]),
        )
        for flip in range(1, 8)
    ]

    def begin(k):
        direct_x(k).start()
        direct_y(k).start()
        side(k).start()

    begin(0)
    for one in square_hops:
        one.start()
    for one in tone_hops[:3]:
        one.start()
    begin(1)

    def spread(k, parity, more):
        direct_x(k).wait_recv()
        if parity == 0:
            far(k, parity).start()
        side_x(k).start()
        direct_y(k).wait_recv()
        if parity == 1:
            far(k, parity).start()
        side_y(k).start()
        if more:
            begin(k + 2)

    def key_copy(k, d):
        return remote(
            heads.at[mates[d], pl.ds(1, 2), at_rows(k)],
            source_ref.at[ctx, pl.ds(1, 2), at_rows(k)],
            key_send.at[d - 1, k],
            key_recv.at[d - 1, k],
            (mates[d], me),
        )

    def late_copy(kind, d):
        source, target = {
            0: (heads.at[mates[d], 0], source_ref.at[ctx, 0]),
            1: (
                tones.at[aligned(ctx * audio_rows, audio_rows)],
                tones.at[aligned(ctx * audio_rows, audio_rows)],
            ),
            2: (parts.at[mates[d]], parts_in.at[ctx]),
            3: (stats.at[mates[d]], stats_in.at[ctx]),
        }[kind]
        return remote(
            source, target, late_send.at[kind, d - 1], late_recv.at[kind, d - 1], (mates[d], me)
        )

    def video_rate(k):
        sums = jnp.sum(every_square[:, pl.ds(k, 1), :], axis=0)
        return to_column(lax.rsqrt(sums / (8 * width) + EPSILON), CHUNK)

    def project(k):
        at = at_rows(k)
        side(k).wait_recv()
        side_x(k).wait_recv()
        side_y(k).wait_recv()
        side_far(k).wait_recv()
        rate = video_rate(k)

        def one(i, carry):
            plane = (i + 1) % 3
            acc = jnp.dot(xs[at, :], w_self[plane], preferred_element_type=F32)
            scaled = (acc * rate).astype(BF16)
            for h in range(local_heads):
                heads[h, plane, at] = scaled[:, h * HD : (h + 1) * HD]
            return carry

        lax.fori_loop(0, 2, one, 0)
        for d in range(1, ctx_size):
            key_copy(k, d).start()
        lax.fori_loop(2, 3, one, 0)
        for plane in range(3):
            source_ref[ctx, plane, at] = heads[ctx, plane, at]

        def other(plane, carry):
            acc = jnp.dot(xs[at, :], w_cross[plane], preferred_element_type=F32)
            scaled = (acc * rate).astype(BF16)
            for h in range(cross_heads):
                cross[h, plane, at] = scaled[:, h * HD : (h + 1) * HD]
            return carry

        lax.fori_loop(0, 3, other, 0)

    def advance(k, parity, more):
        @pl.when(k + 1 < count)
        def _():
            spread(k + 1, 1 - parity, False)

            @pl.when(k + 3 < count)
            def _():
                begin(k + 3)

        far(k, parity).wait_recv()
        side_far(k).start()
        project(k)

    spread(0, 0, True)
    for one in square_hops:
        one.wait_recv()
    loads[1].wait()
    loads[2].wait()
    loads[0].wait()
    load_cross.wait()

    def sing():
        tone_hops[0].wait_recv()
        tone_hops[3].start()
        tone_hops[4].start()
        tone_hops[1].wait_recv()
        tone_hops[5].start()
        load_audio.wait()
        sums = jnp.sum(every_square[:, count : count + 1, :], axis=0)
        rate = to_column(lax.rsqrt(sums / (8 * audio_width) + EPSILON), audio_rows)
        tone_hops[3].wait_recv()
        tone_hops[6].start()
        for slot in (2, 4, 5, 6):
            tone_hops[slot].wait_recv()
        at = aligned(ctx * audio_rows, audio_rows)
        for plane in range(3):
            acc = jnp.dot(xa[...], w_audio[plane], preferred_element_type=F32)
            tones[at, plane * cross_width : (plane + 1) * cross_width] = (acc * rate).astype(BF16)
        for d in range(1, ctx_size):
            late_copy(1, d).start()

    advance(0, 0, True)
    sing()
    advance(1, 1, True)

    def two(i, carry):
        advance(2 * i, 0, True)
        advance(2 * i + 1, 1, True)
        return carry

    lax.fori_loop(1, count // 2, two, 0)
    for d in range(1, ctx_size):
        late_copy(0, d).start()

    for d in range(1, ctx_size):
        late_copy(1, d).wait_recv()
    sound_tile = math.gcd(rows, 256)
    for h in range(cross_heads):
        at = [
            slice(plane * cross_width + h * HD, plane * cross_width + (h + 1) * HD)
            for plane in range(3)
        ]
        own = slice(h * HD, (h + 1) * HD)

        def answer(d, carry):
            query = tones[aligned(d * audio_rows, audio_rows), at[0]]
            mixed, total, highest = softmax_parts(query, [cross[h, 1]], [cross[h, 2]])
            parts[d, :, own] = (mixed / total).astype(BF16)
            stats[d, 2 * h : 2 * h + 1] = to_row(total)
            stats[d, 2 * h + 1 : 2 * h + 2] = to_row(highest)
            return carry

        lax.fori_loop(0, ctx_size, answer, 0)
    for d in range(1, ctx_size):
        late_copy(2, d).start()
        late_copy(3, d).start()
    parts_in[ctx] = parts[ctx]
    stats_in[ctx] = stats[ctx]
    for h in range(cross_heads):
        at = [
            slice(plane * cross_width + h * HD, plane * cross_width + (h + 1) * HD)
            for plane in range(3)
        ]
        own = slice(h * HD, (h + 1) * HD)

        def ask(i, carry):
            tile = aligned(i * sound_tile, sound_tile)
            mixed, total, _ = softmax_parts(cross[h, 0, tile], [tones[:, at[1]]], [tones[:, at[2]]])
            cross_out_ref[tile, own] = (mixed / total).astype(BF16)
            return carry

        lax.fori_loop(0, rows // sound_tile, ask, 0)

    for d in range(1, ctx_size):
        late_copy(2, d).wait_recv()
        late_copy(3, d).wait_recv()
    for h in range(cross_heads):
        own = slice(h * HD, (h + 1) * HD)
        totals = [stats_in[s, 2 * h : 2 * h + 1] for s in range(ctx_size)]
        highs = [stats_in[s, 2 * h + 1 : 2 * h + 2] for s in range(ctx_size)]
        top = functools.reduce(jnp.maximum, highs)
        shares = [total * jnp.exp2(high - top) for total, high in zip(totals, highs)]
        whole = functools.reduce(jnp.add, shares)
        mixed = 0.0
        for s in range(ctx_size):
            share = to_column(shares[s] / whole, audio_rows)
            mixed = mixed + parts_in[s, :, own].astype(F32) * share
        sound_ref[:, own] = mixed.astype(BF16)

    def finish(k, carry):
        for d in range(1, ctx_size):
            key_copy(k, d).wait()
        direct_x(k).wait_send()
        direct_y(k).wait_send()
        for one in (side(k), far(k, 0), side_x(k), side_y(k), side_far(k)):
            one.wait_send()
        return carry

    lax.fori_loop(0, count, finish, 0)
    for d in range(1, ctx_size):
        late_copy(0, d).wait()
        for kind in (1, 2, 3):
            late_copy(kind, d).wait_send()
    for one in tone_hops + square_hops:
        one.wait_send()


def entry(ctx_size, video, audio, video_gain, audio_gain, video_qkv, video_cross, audio_cross):
    rows, width = video.shape
    audio_rows, audio_width = audio.shape
    depth = video_qkv.shape[0]
    audio_depth = audio_cross.shape[0]
    cross_width = video_cross.shape[2]
    count = rows // CHUNK
    local_heads = width // HD
    cross_heads = cross_width // HD
    lines = (count + 1 + 7) // 8 * 8
    vmem = pl.BlockSpec(memory_space=pltpu.VMEM)
    anywhere = pl.BlockSpec(memory_space=pl.ANY)
    dma = pltpu.SemaphoreType.DMA
    others = ctx_size - 1
    return pl.pallas_call(
        functools.partial(entry_kernel, ctx_size),
        out_shape=(
            jax.ShapeDtypeStruct((ctx_size, 3, rows, HD), BF16),
            jax.ShapeDtypeStruct((rows, cross_width), BF16),
            jax.ShapeDtypeStruct((audio_rows, cross_width), BF16),
        ),
        in_specs=[vmem] * 4 + [anywhere] * 3,
        out_specs=(vmem, vmem, vmem),
        scratch_shapes=[
            pltpu.VMEM((rows, depth), BF16),
            pltpu.VMEM((audio_rows, audio_depth), BF16),
            pltpu.VMEM((lines, HD), F32),
            pltpu.VMEM((8, lines, HD), F32),
            pltpu.VMEM((3, depth, width), BF16),
            pltpu.VMEM((3, depth, cross_width), BF16),
            pltpu.VMEM((3, audio_depth, cross_width), BF16),
            pltpu.VMEM((local_heads, 3, rows, HD), BF16),
            pltpu.VMEM((cross_heads, 3, rows, HD), BF16),
            pltpu.VMEM((ctx_size * audio_rows, 3 * cross_width), BF16),
            pltpu.VMEM((ctx_size, audio_rows, cross_width), BF16),
            pltpu.VMEM((ctx_size, audio_rows, cross_width), BF16),
            pltpu.VMEM((ctx_size, 8, HD), F32),
            pltpu.VMEM((ctx_size, 8, HD), F32),
            dma((5,)),
            dma((7, count)),
            dma((7, count)),
            dma((7,)),
            dma((7,)),
            dma((7,)),
            dma((7,)),
            dma((others, count)),
            dma((others, count)),
            dma((4, others)),
            dma((4, others)),
        ],
        compiler_params=pltpu.CompilerParams(
            collective_id=0, has_side_effects=True, vmem_limit_bytes=VMEM_LIMIT
        ),
        name="entry",
    )(
        video,
        audio,
        video_gain.reshape(1, -1),
        audio_gain.reshape(1, -1),
        video_qkv.transpose(1, 0, 2),
        video_cross.transpose(1, 0, 2),
        audio_cross.transpose(1, 0, 2),
    )


def exit_kernel(
    ctx_size,
    source_ref,
    cross_ref,
    sound_ref,
    video_ref,
    audio_ref,
    w_self_ref,
    w_cross_ref,
    w_audio_ref,
    video_out_ref,
    audio_out_ref,
    w_self,
    w_cross,
    w_audio,
    own,
    mixed_out,
    part,
    chip,
    landed,
    tone_part,
    tone_chip,
    tone_landed,
    load,
    back_send,
    back_recv,
    side_send,
    side_recv,
    hop_send,
    hop_recv,
    tone_send,
    tone_recv,
):
    ctx = lax.axis_index("ctx")
    me = lax.axis_index("head")
    rows, width = video_ref.shape
    count = rows // CHUNK
    peer = [head_peer(me, flip) for flip in range(8)]
    mates = [(ctx + d) % ctx_size for d in range(ctx_size)]
    load_audio = pltpu.make_async_copy(w_audio_ref, w_audio, load.at[0])
    load_self = pltpu.make_async_copy(w_self_ref, w_self, load.at[1])
    load_cross = pltpu.make_async_copy(w_cross_ref, w_cross, load.at[2])
    for one in (load_audio, load_self, load_cross):
        one.start()
    barrier = pltpu.get_barrier_semaphore()
    friends = [(ctx, peer[flip]) for flip in (1, 2, 4)]
    friends += [(mates[d], me) for d in range(1, ctx_size)]
    for friend in friends:
        pl.semaphore_signal(barrier, inc=1, device_id=friend, device_id_type=MESH)

    def at_rows(k):
        return aligned(k * CHUNK, CHUNK)

    def reducer(part, chip, landed, at, sems, out_ref, base_ref, parity):
        side_sems, hop_sems = sems
        near_flip, end_flip = (4, 2) if parity else (2, 4)
        near, end = near_flip // 2, end_flip // 2

        def side(i):
            return remote(
                part.at[peer[2 * i + 1], at], chip.at[i, at], *side_sems(i), (ctx, peer[1])
            )

        def hop(slot, flip, k):
            return remote(chip.at[k, at], landed.at[slot, at], *hop_sems(slot), (ctx, peer[flip]))

        def far_hop():
            return hop(0, near_flip, 3)

        def near_hop():
            return hop(1, near_flip, near)

        def end_hop():
            return hop(2, end_flip, end)

        def start():
            for i in (3, near, end, 0):
                side(i).start()

        def fold(i):
            side(i).wait_recv()
            chip[i, at] = (chip[i, at].astype(F32) + part[peer[2 * i], at].astype(F32)).astype(BF16)

        def join():
            fold(3)
            far_hop().start()
            fold(near)
            near_hop().start()
            fold(end)

        def pass_on():
            far_hop().wait_recv()
            chip[end, at] = (chip[end, at].astype(F32) + landed[0, at].astype(F32)).astype(BF16)
            end_hop().start()

        def close():
            side(0).wait_recv()
            total = chip[0, at].astype(F32) + part[me, at].astype(F32) + base_ref[at].astype(F32)
            near_hop().wait_recv()
            total = total + landed[1, at].astype(F32)
            end_hop().wait_recv()
            out_ref[at] = (total + landed[2, at].astype(F32)).astype(BF16)

        def settle():
            for i in range(4):
                side(i).wait_send()
            for one in (far_hop(), near_hop(), end_hop()):
                one.wait_send()

        return start, join, pass_on, close, settle

    def video_steps(k, parity):
        sems = (
            lambda i: (side_send.at[i, k], side_recv.at[i, k]),
            lambda slot: (hop_send.at[slot, k], hop_recv.at[slot, k]),
        )
        return reducer(part, chip, landed, at_rows(k), sems, video_out_ref, video_ref, parity)

    tone_steps = reducer(
        tone_part,
        tone_chip,
        tone_landed,
        pl.ds(0, audio_ref.shape[0]),
        (
            lambda i: (tone_send.at[i], tone_recv.at[i]),
            lambda slot: (tone_send.at[4 + slot], tone_recv.at[4 + slot]),
        ),
        audio_out_ref,
        audio_ref,
        0,
    )

    load_audio.wait()
    tone_width = audio_ref.shape[1]
    for n in range(8):
        tone_part[n] = jnp.dot(
            sound_ref[...],
            w_audio[:, n * tone_width : (n + 1) * tone_width],
            preferred_element_type=F32,
        ).astype(BF16)
    pl.semaphore_wait(barrier, len(friends))
    tone_steps[0]()

    def back(k, d):
        return remote(
            own.at[mates[d], at_rows(k)],
            mixed_out.at[ctx, at_rows(k)],
            back_send.at[d - 1, k],
            back_recv.at[d - 1, k],
            (mates[d], me),
        )

    keys = [source_ref.at[s, 1] for s in range(ctx_size)]
    values = [source_ref.at[s, 2] for s in range(ctx_size)]

    def attend_pair(k, first):
        at = at_rows(k)
        pair = [mates[(first + i) % ctx_size] for i in range(2)]
        query = jnp.concatenate([source_ref[s, 0, at] for s in pair], axis=0)
        mixed, total, _ = softmax_parts(
            query, [key[...] for key in keys], [value[...] for value in values]
        )
        done = (mixed / total).astype(BF16)
        for i, s in enumerate(pair):
            own[s, at] = done[i * CHUNK : (i + 1) * CHUNK]
            d = (first + i) % ctx_size
            if d:
                back(k, d).start()
            else:
                mixed_out[ctx, at] = done[i * CHUNK : (i + 1) * CHUNK]

    def output(k):
        at = at_rows(k)
        for d in range(1, ctx_size):
            back(k, d).wait_recv()
        selfs = jnp.concatenate([mixed_out[s, at] for s in range(ctx_size)], axis=1)

        def one(n, carry):
            cols = aligned(n * width, width)
            part[n, at] = (
                jnp.dot(selfs, w_self[:, cols], preferred_element_type=F32)
                + jnp.dot(cross_ref[at], w_cross[:, cols], preferred_element_type=F32)
            ).astype(BF16)
            return carry

        lax.fori_loop(0, 8, one, 0)
        video_steps(k, 0)[0]()

    def turn(k, parity):
        attend_pair(k, 1)

        @pl.when(k >= 2)
        def _():
            video_steps(k - 2, parity)[2]()

        @pl.when(k >= 1)
        def _():
            output(k - 1)

        attend_pair(k, 3)

        @pl.when(k >= 1)
        def _():
            video_steps(k - 1, 1 - parity)[1]()

        @pl.when(k >= 3)
        def _():
            video_steps(k - 3, 1 - parity)[3]()

    def two(i, carry):
        turn(2 * i, 0)

        @pl.when(i == 0)
        def _():
            tone_steps[1]()
            load_self.wait()
            load_cross.wait()

        turn(2 * i + 1, 1)

        @pl.when(i == 0)
        def _():
            tone_steps[2]()

        return carry

    lax.fori_loop(0, count // 2, two, 0)
    last = count - 1
    video_steps(last - 1, 0)[2]()
    output(last)
    video_steps(last, 1)[1]()
    tone_steps[3]()
    video_steps(last - 2, 1)[3]()
    video_steps(last - 1, 0)[3]()
    video_steps(last, 1)[2]()
    video_steps(last, 1)[3]()

    def finish(k, carry):
        for d in range(1, ctx_size):
            back(k, d).wait_send()
        video_steps(k, 0)[4]()
        return carry

    lax.fori_loop(0, count, finish, 0)
    tone_steps[4]()


def leave(ctx_size, sources, cross_out, sound, video, audio, w_self, w_cross, w_audio):
    rows, width = video.shape
    audio_rows, audio_width = audio.shape
    count = rows // CHUNK
    vmem = pl.BlockSpec(memory_space=pltpu.VMEM)
    anywhere = pl.BlockSpec(memory_space=pl.ANY)
    dma = pltpu.SemaphoreType.DMA
    others = ctx_size - 1
    return pl.pallas_call(
        functools.partial(exit_kernel, ctx_size),
        out_shape=(
            jax.ShapeDtypeStruct(video.shape, BF16),
            jax.ShapeDtypeStruct(audio.shape, BF16),
        ),
        in_specs=[vmem] * 5 + [anywhere] * 3,
        out_specs=(vmem, vmem),
        scratch_shapes=[
            pltpu.VMEM(w_self.shape, BF16),
            pltpu.VMEM(w_cross.shape, BF16),
            pltpu.VMEM(w_audio.shape, BF16),
            pltpu.VMEM((ctx_size, rows, HD), BF16),
            pltpu.VMEM((ctx_size, rows, HD), BF16),
            pltpu.VMEM((8, rows, width), BF16),
            pltpu.VMEM((4, rows, width), BF16),
            pltpu.VMEM((3, rows, width), BF16),
            pltpu.VMEM((8, audio_rows, audio_width), BF16),
            pltpu.VMEM((4, audio_rows, audio_width), BF16),
            pltpu.VMEM((3, audio_rows, audio_width), BF16),
            dma((3,)),
            dma((others, count)),
            dma((others, count)),
            dma((4, count)),
            dma((4, count)),
            dma((3, count)),
            dma((3, count)),
            dma((7,)),
            dma((7,)),
        ],
        compiler_params=pltpu.CompilerParams(
            collective_id=1, has_side_effects=True, vmem_limit_bytes=VMEM_LIMIT
        ),
        name="leave",
    )(sources, cross_out, sound, video, audio, w_self, w_cross, w_audio)


def fast_body(
    ctx_size,
    video,
    audio,
    video_gain,
    audio_gain,
    video_qkv,
    video_cross,
    audio_cross,
    video_out,
    cross_video_out,
    cross_audio_out,
):
    sources, cross_out, sound = entry(
        ctx_size, video, audio, video_gain, audio_gain, video_qkv, video_cross, audio_cross
    )
    return leave(
        ctx_size,
        sources,
        cross_out,
        sound,
        video,
        audio,
        video_out,
        cross_video_out,
        cross_audio_out,
    )


def suits(ctx_size, head_size, video, audio, video_cross):
    rows, width = video.shape
    audio_rows, audio_width = audio.shape
    return (
        head_size == 8
        and ctx_size == 4
        and width == ctx_size * HD
        and rows % (2 * CHUNK) == 0
        and rows >= 4 * CHUNK
        and audio_rows % 16 == 0
        and audio_rows <= HD
        and audio_width % HD == 0
        and video_cross.shape[2] % HD == 0
        and video_cross.shape[2] <= 4 * HD
    )


def solution(mesh):
    ctx_size = mesh.shape["ctx"]

    def body(*operands):
        if suits(ctx_size, mesh.shape["head"], operands[0], operands[1], operands[5]):
            return fast_body(ctx_size, *operands)
        return plain_body(*operands)

    return jax.shard_map(
        body,
        mesh=mesh,
        in_specs=(
            P("ctx", "head"),
            P("ctx", "head"),
            P("head"),
            P("head"),
            P(None, None, "head"),
            P(None, None, "head"),
            P(None, None, "head"),
            P("head", None),
            P("head", None),
            P("head", None),
        ),
        out_specs=(P("ctx", "head"), P("ctx", "head")),
        check_vma=False,
    )
```

profile of v0, /device:TPU:0, one launch (start us, length us, event | category | flops | bytes accessed | tf_op | source)
XLA Modules:
  0.0 168.1 jit_solution(5664027952924753024)
XLA Ops:
  0.6 94.7 %entry.1 = (bf16[4,3,768,128]{3,2,1,0:T(8,128)(2,1)}, bf16[768,256]{1,0:T(8,128)(2,1)}, bf16[96,256]{1,0:T(8,128)(2,1)}) custom-call(bf16[768,512]{1,0:T(8,128)(2,1)} %video_ref.3, bf16[96,256]{1,0:T(8,128)(2,1)} %audio_ref.3, f32[1,512]{1,0:T(1,128)} %bitcast.8, f32[1,256]{1,0:T(1,128)} %bitcast.9, bf16[3,4096,512]{2,1,0:T(8,128)(2,1)} %bitcast.5, ...), custom_call_target="tpu_custom_call" | custom-call | tf_op jit(solution)/shard_map/entry/pallas_call | solution.py:589
  95.3 69.3 %leave.1 = (bf16[768,512]{1,0:T(8,128)(2,1)}, bf16[96,256]{1,0:T(8,128)(2,1)}) custom-call(bf16[4,3,768,128]{3,2,1,0:T(8,128)(2,1)} %get-tuple-element.5.source_ref, bf16[768,256]{1,0:T(8,128)(2,1)} %get-tuple-element.6.cross_ref, bf16[96,256]{1,0:T(8,128)(2,1)} %get-tuple-element.7.sound_ref, bf16[768,512]{1,0:T(8,128)(2,1)} %video_ref.3, ...), custom_call_target="tpu_custom_call" | custom-call | tf_op jit(solution)/shard_map/leave/pallas_call | solution.py:895
  164.6 2.1 %copy.14 = bf16[768,512]{1,0:T(8,128)(2,1)} copy(bf16[768,512]{1,0:T(8,128)(2,1)} %get-tuple-element.10) | data formatting | bytes 1572864
  166.7 1.4 copy.15
where the time goes:
time: 168 us
  Pallas kernels  164 us (98%)
  local copies, waits for them, and re-layouts  3.48 us (2%)
    pallas_call x1, Pallas kernels, entry(): pl.pallas_call(functools.partial(entry_kernel, ctx_size), out_shape=(jax....  94.7 us
    pallas_call x1, Pallas kernels, leave(): pl.pallas_call(functools.partial(exit_kernel, ctx_size), out_shape=(jax.S...  69.3 us
    unnamed x2, local copies, waits for them, and re-layouts  3.48 us

commit v1 on v0

v1 whole, which is shorter than its diff:
```python
import functools
import math

import jax
import jax.numpy as jnp
from jax import lax
from jax.experimental import pallas as pl
from jax.experimental.pallas import tpu as pltpu

from jax.sharding import PartitionSpec as P

HD = 128


EPSILON = 1e-06


def split_heads(matrix):
    return matrix.reshape(matrix.shape[0], -1, HD).transpose(1, 0, 2)


def join_heads(blocks):
    return blocks.transpose(1, 0, 2).reshape(blocks.shape[1], -1)


def attend(queries, keys, values):
    scale = HD ** (-0.5)

    def one_head(operands):
        query_block, key_block, value_block = operands
        scores = jnp.dot(query_block, key_block.T, preferred_element_type=jnp.float32) * scale
        highest = jnp.max(scores, axis=1, keepdims=True)
        weights = jnp.exp(scores - highest)
        totals = jnp.sum(weights, axis=1, keepdims=True)
        return (
            jnp.dot(weights.astype(jnp.bfloat16), value_block, preferred_element_type=jnp.float32)
            / totals
        )

    blocks = lax.map(one_head, (split_heads(queries), split_heads(keys), split_heads(values)))
    return join_heads(blocks).astype(jnp.bfloat16)


def plain_body(
    video,
    audio,
    video_gain,
    audio_gain,
    video_qkv,
    video_cross,
    audio_cross,
    video_out,
    cross_video_out,
    cross_audio_out,
):
    scale = HD ** (-0.5)
    video_wide = video.astype(jnp.float32)
    audio_wide = audio.astype(jnp.float32)
    video_squares, audio_squares = lax.psum(
        (jnp.sum(video_wide * video_wide, axis=1), jnp.sum(audio_wide * audio_wide, axis=1)), "head"
    )
    video_rate = lax.rsqrt(video_squares / video_qkv.shape[0] + EPSILON)
    audio_rate = lax.rsqrt(audio_squares / audio_cross.shape[0] + EPSILON)
    video_scaled = (video_wide * video_gain).astype(jnp.bfloat16)
    audio_scaled = (audio_wide * audio_gain).astype(jnp.bfloat16)
    self_weight = video_qkv.reshape(video_qkv.shape[0], -1)
    mixed_weight = video_cross.reshape(video_cross.shape[0], -1)
    audio_weight = audio_cross.reshape(audio_cross.shape[0], -1)
    self_width = video_qkv.shape[2]
    cross_width = video_cross.shape[2]
    video_rows = video.shape[0]
    segment = lax.all_gather(video_scaled, "head", axis=1, tiled=True)
    self_acc = jnp.dot(segment, self_weight, preferred_element_type=jnp.float32)
    mixed_acc = jnp.dot(segment, mixed_weight, preferred_element_type=jnp.float32)
    audio_acc = jnp.dot(
        lax.all_gather(audio_scaled, "head", axis=1, tiled=True),
        audio_weight,
        preferred_element_type=jnp.float32,
    )
    self_proj = (self_acc * video_rate[:, None]).astype(jnp.bfloat16)
    video_mixed = (mixed_acc * video_rate[:, None]).astype(jnp.bfloat16)
    audio_mixed = (audio_acc * audio_rate[:, None]).astype(jnp.bfloat16)
    query_heads = split_heads(self_proj[:, :self_width])
    local_heads = query_heads.shape[0]
    running_max = jnp.full((local_heads, video_rows), -1e30, jnp.float32)
    key_heads = split_heads(
        lax.all_gather(self_proj[:, self_width : 2 * self_width], "ctx", axis=0, tiled=True)
    )
    value_heads = split_heads(
        lax.all_gather(self_proj[:, 2 * self_width :], "ctx", axis=0, tiled=True)
    )
    scores = (
        jnp.einsum("hqd,hkd->hqk", query_heads, key_heads, preferred_element_type=jnp.float32)
        * scale
    )
    newest = jnp.maximum(running_max, jnp.max(scores, axis=2))
    weights = jnp.exp(scores - newest[:, :, None])
    running_sum = jnp.sum(weights, axis=2)
    running_acc = jnp.einsum(
        "hqk,hkd->hqd",
        weights.astype(jnp.bfloat16),
        value_heads,
        preferred_element_type=jnp.float32,
    )
    self_out = join_heads(running_acc / running_sum[:, :, None]).astype(jnp.bfloat16)
    audio_key_all, audio_value_all = (
        lax.all_gather(audio_mixed[:, cross_width : 2 * cross_width], "ctx", axis=0, tiled=True),
        lax.all_gather(audio_mixed[:, 2 * cross_width :], "ctx", axis=0, tiled=True),
    )
    video_cross_out = attend(video_mixed[:, :cross_width], audio_key_all, audio_value_all)
    queries_av = audio_mixed[:, :cross_width]
    keys_av = video_mixed[:, cross_width : 2 * cross_width]
    values_av = video_mixed[:, 2 * cross_width :]
    every_query = lax.all_gather(queries_av, "ctx", axis=0, tiled=True)
    scores = (
        jnp.einsum(
            "hqd,hkd->hqk",
            split_heads(every_query),
            split_heads(keys_av),
            preferred_element_type=jnp.float32,
        )
        * scale
    )
    highest = lax.pmax(jnp.max(scores, axis=2), "ctx")
    weights = jnp.exp(scores - highest[:, :, None])
    numerators = jnp.einsum(
        "hqk,hkd->hqd",
        weights.astype(jnp.bfloat16),
        split_heads(values_av),
        preferred_element_type=jnp.float32,
    )
    weight_totals = jnp.sum(weights, axis=2)
    own_numer, own_totals = (
        lax.psum_scatter(
            numerators.astype(jnp.bfloat16), "ctx", scatter_dimension=1, tiled=True
        ).astype(jnp.float32),
        lax.psum_scatter(
            weight_totals.astype(jnp.bfloat16), "ctx", scatter_dimension=1, tiled=True
        ).astype(jnp.float32),
    )
    audio_cross_out = join_heads(own_numer / own_totals[:, :, None]).astype(jnp.bfloat16)
    video_partial = jnp.dot(self_out, video_out, preferred_element_type=jnp.float32) + jnp.dot(
        video_cross_out, cross_video_out, preferred_element_type=jnp.float32
    )
    audio_partial = jnp.dot(audio_cross_out, cross_audio_out, preferred_element_type=jnp.float32)
    video_sum, audio_sum = (
        lax.psum_scatter(
            video_partial.astype(jnp.bfloat16), "head", scatter_dimension=1, tiled=True
        ).astype(jnp.float32),
        lax.psum_scatter(
            audio_partial.astype(jnp.bfloat16), "head", scatter_dimension=1, tiled=True
        ).astype(jnp.float32),
    )
    return (
        (video_wide + video_sum).astype(jnp.bfloat16),
        (audio_wide + audio_sum).astype(jnp.bfloat16),
    )


MESH = pl.DeviceIdType.MESH
F32 = jnp.float32
BF16 = jnp.bfloat16
VMEM_LIMIT = 63 * 1024 * 1024
CHUNK = HD
SCORE_SCALE = HD ** (-0.5) * math.log2(math.e)


def head_peer(me, flip):
    low = me % 2
    mid = (me // 2) % 2
    high = me // 4
    if flip & 1:
        low = 1 - low
    if flip & 2:
        mid = 1 - mid
    if flip & 4:
        high = 1 - high
    return high * 4 + mid * 2 + low


def remote(source, target, send, recv, device):
    return pltpu.make_async_remote_copy(
        src_ref=source,
        dst_ref=target,
        send_sem=send,
        recv_sem=recv,
        device_id=device,
        device_id_type=MESH,
    )


def diagonal(rows):
    line = lax.broadcasted_iota(jnp.int32, (rows, HD), 0)
    lane = lax.broadcasted_iota(jnp.int32, (rows, HD), 1)
    return line == lane


def to_row(column):
    rows = column.shape[0]
    spread = jnp.broadcast_to(column, (rows, HD))
    return jnp.sum(jnp.where(diagonal(rows), spread, 0.0), axis=0, keepdims=True)


def to_column(row, rows):
    spread = jnp.broadcast_to(row, (rows, HD))
    return jnp.sum(jnp.where(diagonal(rows), spread, 0.0), axis=1, keepdims=True)


def contract_last(left, right):
    return lax.dot_general(left, right, (((1,), (1,)), ((), ())), preferred_element_type=F32)


def softmax_parts(query, keys, values):
    scores = [contract_last(query, key) for key in keys]
    highest = functools.reduce(
        jnp.maximum, [jnp.max(score, axis=1, keepdims=True) for score in scores]
    )
    total = 0.0
    mixed = 0.0
    for score, value in zip(scores, values):
        weight = jnp.exp2((score - highest) * SCORE_SCALE)
        total = total + jnp.sum(weight, axis=1, keepdims=True)
        mixed = mixed + jnp.dot(weight.astype(BF16), value, preferred_element_type=F32)
    return mixed, total, highest * SCORE_SCALE


def aligned(start, size):
    return pl.ds(pl.multiple_of(start, size), size)


def block_kernel(
    ctx_size,
    video_ref,
    audio_ref,
    video_gain_ref,
    audio_gain_ref,
    w_self_ref,
    w_cross_ref,
    w_audio_ref,
    w_out_ref,
    w_cross_out_ref,
    w_audio_out_ref,
    video_out_ref,
    audio_out_ref,
    xs,
    xa,
    raw,
    squares,
    every_square,
    tone_squares,
    every_tone_square,
    w_self,
    w_cross,
    w_audio,
    w_out,
    w_cross_out,
    w_audio_out,
    heads,
    sources,
    cross,
    cross_out,
    tones,
    parts,
    parts_in,
    stats,
    stats_in,
    own,
    mixed_out,
    chip,
    landed,
    tone_part,
    tone_chip,
    tone_landed,
    load,
    plane_send,
    plane_recv,
    tone_send,
    tone_recv,
    square_send,
    square_recv,
    key_send,
    key_recv,
    query_send,
    query_recv,
    back_send,
    back_recv,
    late_send,
    late_recv,
    side_send,
    side_recv,
    hop_send,
    hop_recv,
    tone_out_send,
    tone_out_recv,
):
    ctx = lax.axis_index("ctx")
    me = lax.axis_index("head")
    rows, width = video_ref.shape
    audio_rows, audio_width = audio_ref.shape
    every_tone = ctx_size * audio_rows
    count = rows // CHUNK
    local_heads = width // HD
    cross_width = w_cross.shape[2]
    cross_heads = cross_width // HD
    peer = [head_peer(me, flip) for flip in range(8)]
    mates = [(ctx + d) % ctx_size for d in range(ctx_size)]
    others = range(1, ctx_size)

    def loader(slot, source, target):
        return pltpu.make_async_copy(source, target, load.at[slot])

    loads = [
        loader(0, w_self_ref.at[1], w_self.at[1]),
        loader(1, w_self_ref.at[2], w_self.at[2]),
        loader(2, w_self_ref.at[0], w_self.at[0]),
        loader(3, w_cross_ref, w_cross),
        loader(4, w_audio_ref, w_audio),
        loader(5, w_out_ref, w_out),
        loader(6, w_cross_out_ref, w_cross_out),
        loader(7, w_audio_out_ref, w_audio_out),
    ]
    for one in loads:
        one.start()

    barrier = pltpu.get_barrier_semaphore()
    friends = [(ctx, peer[flip]) for flip in range(1, 8)]
    friends += [(mates[d], me) for d in others]
    for friend in friends:
        pl.semaphore_signal(barrier, inc=1, device_id=friend, device_id_type=MESH)

    def at_rows(k):
        return aligned(k * CHUNK, CHUNK)

    def columns(block):
        return aligned(block * width, width)

    def tone_columns(block):
        return aligned(block * audio_width, audio_width)

    my_tones = aligned(ctx * audio_rows, audio_rows)
    for k in range(count):
        wide = video_ref[pl.ds(k * CHUNK, CHUNK)].astype(F32)
        xs[pl.ds(k * CHUNK, CHUNK), columns(me)] = (wide * video_gain_ref[...]).astype(BF16)
        squares[k : k + 1] = to_row(jnp.sum(wide * wide, axis=1, keepdims=True))
    every_square[0] = squares[...]
    raw[my_tones] = audio_ref[...]

    pl.semaphore_wait(barrier, len(friends))

    def hop(slot, k):
        flip, block = (slot, me) if slot in (1, 2, 4, 6) else (1, peer[slot - 1])
        part = xs.at[at_rows(k), columns(block)]
        return remote(
            part, part, plane_send.at[slot - 1, k], plane_recv.at[slot - 1, k], (ctx, peer[flip])
        )

    def tone_hop(slot):
        flip, block = (slot, me) if slot in (1, 2, 4, 6) else (1, peer[slot - 1])
        part = xa.at[:, tone_columns(block)]
        return remote(
            part, part, tone_send.at[slot - 1], tone_recv.at[slot - 1], (ctx, peer[flip])
        )

    def square_hop(kind, flip):
        source, target = (
            (tone_squares, every_tone_square) if kind else (squares, every_square)
        )
        return remote(
            source,
            target.at[flip],
            square_send.at[kind, flip - 1],
            square_recv.at[kind, flip - 1],
            (ctx, peer[flip]),
        )

    def late_copy(kind, d):
        source, target = {
            0: (audio_ref, raw.at[my_tones]),
            1: (parts.at[mates[d]], parts_in.at[ctx]),
            2: (stats.at[mates[d]], stats_in.at[ctx]),
        }[kind]
        return remote(
            source, target, late_send.at[kind, d - 1], late_recv.at[kind, d - 1], (mates[d], me)
        )

    def key_copy(k, d):
        return remote(
            heads.at[mates[d], pl.ds(1, 2), at_rows(k)],
            sources.at[ctx, pl.ds(1, 2), at_rows(k)],
            key_send.at[d - 1, k],
            key_recv.at[d - 1, k],
            (mates[d], me),
        )

    def query_copy(k, d):
        return remote(
            heads.at[mates[d], 0, at_rows(k)],
            sources.at[ctx, 0, at_rows(k)],
            query_send.at[d - 1, k],
            query_recv.at[d - 1, k],
            (mates[d], me),
        )

    for d in others:
        late_copy(0, d).start()
    for slot in (6, 2, 4, 1):
        hop(slot, 0).start()
    for flip in range(1, 8):
        square_hop(0, flip).start()

    def begin(k, carry):
        for slot in (6, 2, 4, 1):
            hop(slot, k).start()
        return carry

    lax.fori_loop(1, count, begin, 0)

    for d in others:
        late_copy(0, d).wait_recv()
    tone_squares[...] = jnp.zeros_like(tone_squares)
    for d in range(ctx_size):
        at = pl.ds(d * audio_rows, audio_rows)
        wide = raw[at].astype(F32)
        xa[at, tone_columns(me)] = (wide * audio_gain_ref[...]).astype(BF16)
        tone_squares[d : d + 1] = to_row(jnp.sum(wide * wide, axis=1, keepdims=True))
    every_tone_square[0] = tone_squares[...]
    for one in loads[:4]:
        one.wait()
    for flip in range(1, 8):
        square_hop(0, flip).wait_recv()
    for flip in range(1, 8):
        square_hop(1, flip).start()
    for slot in (6, 2, 4, 1):
        tone_hop(slot).start()

    def video_rate(k):
        sums = jnp.sum(every_square[:, pl.ds(k, 1), :], axis=0)
        return to_column(lax.rsqrt(sums / (8 * width) + EPSILON), CHUNK)

    def cross_project(k):
        at = at_rows(k)
        rate = video_rate(k)

        def one(plane, carry):
            acc = jnp.dot(xs[at, :], w_cross[plane], preferred_element_type=F32)
            scaled = (acc * rate).astype(BF16)
            for h in range(cross_heads):
                cross[h, plane, at] = scaled[:, h * HD : (h + 1) * HD]
            return carry

        lax.fori_loop(0, 3, one, 0)

    def project(k, carry):
        at = at_rows(k)
        for slot in (2, 4, 6):
            hop(slot, k).wait_recv()
            hop(slot + 1, k).start()

        @pl.when(k > 0)
        def _():
            cross_project(k - 1)

        for slot in (1, 3, 5, 7):
            hop(slot, k).wait_recv()
        rate = video_rate(k)

        def one(i, carry):
            plane = (i + 1) % 3
            acc = jnp.dot(xs[at, :], w_self[plane], preferred_element_type=F32)
            scaled = (acc * rate).astype(BF16)
            for h in range(local_heads):
                heads[h, plane, at] = scaled[:, h * HD : (h + 1) * HD]

            @pl.when(i == 1)
            def _():
                for d in others:
                    key_copy(k, d).start()

            return carry

        lax.fori_loop(0, 3, one, 0)
        for plane in range(3):
            sources[ctx, plane, at] = heads[ctx, plane, at]
        return carry

    lax.fori_loop(0, count, project, 0)

    def ship(k, carry):
        for d in others:
            query_copy(k, d).start()
        return carry

    lax.fori_loop(0, count, ship, 0)
    cross_project(count - 1)

    for slot in (2, 4, 6):
        tone_hop(slot).wait_recv()
        tone_hop(slot + 1).start()
    loads[4].wait()
    for flip in range(1, 8):
        square_hop(1, flip).wait_recv()
    for slot in (1, 3, 5, 7):
        tone_hop(slot).wait_recv()
    tone_sums = jnp.sum(every_tone_square[...], axis=0)
    tone_rates = lax.rsqrt(tone_sums / (8 * audio_width) + EPSILON)
    rate = jnp.concatenate(
        [to_column(tone_rates[d : d + 1], audio_rows) for d in range(ctx_size)], axis=0
    )
    for plane in range(3):
        acc = jnp.dot(xa[...], w_audio[plane], preferred_element_type=F32)
        tones[:, plane * cross_width : (plane + 1) * cross_width] = (acc * rate).astype(BF16)

    sound_tile = math.gcd(rows, 256)

    def tone_part_of(plane, h):
        return slice(plane * cross_width + h * HD, plane * cross_width + (h + 1) * HD)

    for h in range(cross_heads):
        lanes = slice(h * HD, (h + 1) * HD)

        def answer(d, carry):
            query = tones[aligned(d * audio_rows, audio_rows), tone_part_of(0, h)]
            mixed, total, highest = softmax_parts(query, [cross[h, 1]], [cross[h, 2]])
            parts[d, :, lanes] = (mixed / total).astype(BF16)
            stats[d, 2 * h : 2 * h + 1] = to_row(total)
            stats[d, 2 * h + 1 : 2 * h + 2] = to_row(highest)
            return carry

        lax.fori_loop(0, ctx_size, answer, 0)
    for d in others:
        late_copy(1, d).start()
        late_copy(2, d).start()
    parts_in[ctx] = parts[ctx]
    stats_in[ctx] = stats[ctx]
    for h in range(cross_heads):
        lanes = slice(h * HD, (h + 1) * HD)

        def ask(i, carry):
            tile = aligned(i * sound_tile, sound_tile)
            mixed, total, _ = softmax_parts(
                cross[h, 0, tile], [tones[:, tone_part_of(1, h)]], [tones[:, tone_part_of(2, h)]]
            )
            cross_out[tile, lanes] = (mixed / total).astype(BF16)
            return carry

        lax.fori_loop(0, rows // sound_tile, ask, 0)

    def settle_hops(k, carry):
        for slot in range(1, 8):
            hop(slot, k).wait_send()
        for d in others:
            key_copy(k, d).wait_recv()
        return carry

    lax.fori_loop(0, count, settle_hops, 0)
    for one in loads[5:]:
        one.wait()

    def reducer(part_at, chip, landed, at, side_sems, hop_sems, out_ref, base_ref, parity):
        near_flip, end_flip = (4, 2) if parity else (2, 4)
        near, end = near_flip // 2, end_flip // 2

        def side(i):
            return remote(
                part_at(peer[2 * i + 1]), chip.at[i, at], *side_sems(i), (ctx, peer[1])
            )

        def hop(slot, flip, k):
            return remote(chip.at[k, at], landed.at[slot, at], *hop_sems(slot), (ctx, peer[flip]))

        def far_hop():
            return hop(0, near_flip, 3)

        def near_hop():
            return hop(1, near_flip, near)

        def end_hop():
            return hop(2, end_flip, end)

        def start():
            for i in (3, near, end, 0):
                side(i).start()

        def fold(i):
            side(i).wait_recv()
            chip[i, at] = (
                chip[i, at].astype(F32) + part_at(peer[2 * i])[...].astype(F32)
            ).astype(BF16)

        def join():
            fold(3)
            far_hop().start()
            fold(near)
            near_hop().start()
            fold(end)

        def pass_on():
            far_hop().wait_recv()
            chip[end, at] = (chip[end, at].astype(F32) + landed[0, at].astype(F32)).astype(BF16)
            end_hop().start()

        def close():
            side(0).wait_recv()
            total = chip[0, at].astype(F32) + part_at(me)[...].astype(F32)
            total = total + base_ref[at].astype(F32)
            near_hop().wait_recv()
            total = total + landed[1, at].astype(F32)
            end_hop().wait_recv()
            out_ref[at] = (total + landed[2, at].astype(F32)).astype(BF16)

        def settle():
            for i in range(4):
                side(i).wait_send()
            for one in (far_hop(), near_hop(), end_hop()):
                one.wait_send()

        return start, join, pass_on, close, settle

    def video_steps(k, parity):
        return reducer(
            lambda block: xs.at[at_rows(k), columns(block)],
            chip,
            landed,
            at_rows(k),
            lambda i: (side_send.at[i, k], side_recv.at[i, k]),
            lambda slot: (hop_send.at[slot, k], hop_recv.at[slot, k]),
            video_out_ref,
            video_ref,
            parity,
        )

    tone_start, tone_join, tone_pass, tone_close, tone_settle = reducer(
        lambda block: tone_part.at[block],
        tone_chip,
        tone_landed,
        pl.ds(0, audio_rows),
        lambda i: (tone_out_send.at[i], tone_out_recv.at[i]),
        lambda slot: (tone_out_send.at[4 + slot], tone_out_recv.at[4 + slot]),
        audio_out_ref,
        audio_ref,
        0,
    )

    def sound():
        for d in others:
            late_copy(1, d).wait_recv()
            late_copy(2, d).wait_recv()
        pieces = []
        for h in range(cross_heads):
            lanes = slice(h * HD, (h + 1) * HD)
            totals = [stats_in[s, 2 * h : 2 * h + 1] for s in range(ctx_size)]
            highs = [stats_in[s, 2 * h + 1 : 2 * h + 2] for s in range(ctx_size)]
            top = functools.reduce(jnp.maximum, highs)
            shares = [total * jnp.exp2(high - top) for total, high in zip(totals, highs)]
            whole = functools.reduce(jnp.add, shares)
            mixed = 0.0
            for s in range(ctx_size):
                share = to_column(shares[s] / whole, audio_rows)
                mixed = mixed + parts_in[s, :, lanes].astype(F32) * share
            pieces.append(mixed.astype(BF16))
        result = jnp.concatenate(pieces, axis=1)
        for n in range(8):
            tone_part[n] = jnp.dot(
                result,
                w_audio_out[:, n * audio_width : (n + 1) * audio_width],
                preferred_element_type=F32,
            ).astype(BF16)
        tone_start()

    def back(k, d):
        return remote(
            own.at[mates[d], at_rows(k)],
            mixed_out.at[ctx, at_rows(k)],
            back_send.at[d - 1, k],
            back_recv.at[d - 1, k],
            (mates[d], me),
        )

    def attend_pair(k, first):
        at = at_rows(k)
        pair = [mates[(first + i) % ctx_size] for i in range(2)]
        query = jnp.concatenate([sources[s, 0, at] for s in pair], axis=0)
        mixed, total, _ = softmax_parts(
            query,
            [sources[s, 1] for s in range(ctx_size)],
            [sources[s, 2] for s in range(ctx_size)],
        )
        done = (mixed / total).astype(BF16)
        for i, s in enumerate(pair):
            own[s, at] = done[i * CHUNK : (i + 1) * CHUNK]
            d = (first + i) % ctx_size
            if d:
                back(k, d).start()
            else:
                mixed_out[ctx, at] = done[i * CHUNK : (i + 1) * CHUNK]

    def output(k):
        at = at_rows(k)
        for d in others:
            back(k, d).wait_recv()
        selfs = jnp.concatenate([mixed_out[s, at] for s in range(ctx_size)], axis=1)

        def one(n, carry):
            cols = columns(n)
            xs[at, cols] = (
                jnp.dot(selfs, w_out[:, cols], preferred_element_type=F32)
                + jnp.dot(cross_out[at], w_cross_out[:, cols], preferred_element_type=F32)
            ).astype(BF16)
            return carry

        lax.fori_loop(0, 8, one, 0)
        video_steps(k, 0)[0]()

    def turn(k, parity):
        for d in others:
            query_copy(k, d).wait_recv()
        attend_pair(k, 1)

        @pl.when(k >= 2)
        def _():
            video_steps(k - 2, parity)[1]()

        attend_pair(k, 3)

        @pl.when(k >= 3)
        def _():
            video_steps(k - 3, 1 - parity)[2]()

        @pl.when(k >= 1)
        def _():
            output(k - 1)

        @pl.when(k >= 4)
        def _():
            video_steps(k - 4, parity)[3]()

    def two(i, carry):
        turn(2 * i, 0)

        @pl.when(i == 1)
        def _():
            sound()

        @pl.when(i == 2)
        def _():
            tone_pass()

        turn(2 * i + 1, 1)

        @pl.when(i == 1)
        def _():
            tone_join()

        return carry

    lax.fori_loop(0, count // 2, two, 0)
    last = count - 1
    video_steps(last - 1, 0)[1]()
    video_steps(last - 2, 1)[2]()
    output(last)
    tone_close()
    video_steps(last, 1)[1]()
    video_steps(last - 1, 0)[2]()
    video_steps(last - 3, 0)[3]()
    video_steps(last - 2, 1)[3]()
    video_steps(last, 1)[2]()
    video_steps(last - 1, 0)[3]()
    video_steps(last, 1)[3]()

    def finish(k, carry):
        for d in others:
            key_copy(k, d).wait_send()
            query_copy(k, d).wait_send()
            back(k, d).wait_send()
        video_steps(k, 0)[4]()
        return carry

    lax.fori_loop(0, count, finish, 0)
    for d in others:
        for kind in range(3):
            late_copy(kind, d).wait_send()
    for slot in range(1, 8):
        tone_hop(slot).wait_send()
    for flip in range(1, 8):
        for kind in range(2):
            square_hop(kind, flip).wait_send()
    tone_settle()


def fast_body(
    ctx_size,
    video,
    audio,
    video_gain,
    audio_gain,
    video_qkv,
    video_cross,
    audio_cross,
    video_out,
    cross_video_out,
    cross_audio_out,
):
    rows, width = video.shape
    audio_rows, audio_width = audio.shape
    depth = video_qkv.shape[0]
    audio_depth = audio_cross.shape[0]
    cross_width = video_cross.shape[2]
    count = rows // CHUNK
    cross_heads = cross_width // HD
    lines = (count + 7) // 8 * 8
    others = ctx_size - 1
    every_tone = ctx_size * audio_rows
    vmem = pl.BlockSpec(memory_space=pltpu.VMEM)
    anywhere = pl.BlockSpec(memory_space=pl.ANY)

    def wide(*shape):
        return pltpu.VMEM(shape, BF16)

    def fine(*shape):
        return pltpu.VMEM(shape, F32)

    def pair(*shape):
        return [pltpu.SemaphoreType.DMA(shape)] * 2

    return pl.pallas_call(
        functools.partial(block_kernel, ctx_size),
        out_shape=(
            jax.ShapeDtypeStruct(video.shape, BF16),
            jax.ShapeDtypeStruct(audio.shape, BF16),
        ),
        in_specs=[vmem] * 4 + [anywhere] * 6,
        out_specs=(vmem, vmem),
        scratch_shapes=[
            wide(rows, depth),
            wide(every_tone, audio_depth),
            wide(every_tone, audio_width),
            fine(lines, HD),
            fine(8, lines, HD),
            fine(8, HD),
            fine(8, 8, HD),
            wide(3, depth, width),
            wide(3, depth, cross_width),
            wide(3, audio_depth, cross_width),
            wide(*video_out.shape),
            wide(*cross_video_out.shape),
            wide(*cross_audio_out.shape),
            wide(ctx_size, 3, rows, HD),
            wide(ctx_size, 3, rows, HD),
            wide(cross_heads, 3, rows, HD),
            wide(rows, cross_width),
            wide(every_tone, 3 * cross_width),
            wide(ctx_size, audio_rows, cross_width),
            wide(ctx_size, audio_rows, cross_width),
            fine(ctx_size, 8, HD),
            fine(ctx_size, 8, HD),
            wide(ctx_size, rows, HD),
            wide(ctx_size, rows, HD),
            wide(4, rows, width),
            wide(3, rows, width),
            wide(8, audio_rows, audio_width),
            wide(4, audio_rows, audio_width),
            wide(3, audio_rows, audio_width),
            pltpu.SemaphoreType.DMA((8,)),
            *pair(7, count),
            *pair(7),
            *pair(2, 7),
            *pair(others, count),
            *pair(others, count),
            *pair(others, count),
            *pair(3, others),
            *pair(4, count),
            *pair(3, count),
            *pair(7),
        ],
        compiler_params=pltpu.CompilerParams(
            collective_id=0, has_side_effects=True, vmem_limit_bytes=VMEM_LIMIT
        ),
        name="block",
    )(
        video,
        audio,
        video_gain.reshape(1, -1),
        audio_gain.reshape(1, -1),
        video_qkv.transpose(1, 0, 2),
        video_cross.transpose(1, 0, 2),
        audio_cross.transpose(1, 0, 2),
        video_out,
        cross_video_out,
        cross_audio_out,
    )


def suits(ctx_size, head_size, video, audio, video_cross):
    rows, width = video.shape
    audio_rows, audio_width = audio.shape
    return (
        head_size == 8
        and ctx_size == 4
        and width == ctx_size * HD
        and rows % (2 * CHUNK) == 0
        and rows >= 6 * CHUNK
        and audio_rows % 16 == 0
        and audio_rows <= HD
        and audio_width % HD == 0
        and video_cross.shape[2] % HD == 0
        and video_cross.shape[2] <= 4 * HD
    )


def solution(mesh):
    ctx_size = mesh.shape["ctx"]

    def body(*operands):
        if suits(ctx_size, mesh.shape["head"], operands[0], operands[1], operands[5]):
            return fast_body(ctx_size, *operands)
        return plain_body(*operands)

    return jax.shard_map(
        body,
        mesh=mesh,
        in_specs=(
            P("ctx", "head"),
            P("ctx", "head"),
            P("head"),
            P("head"),
            P(None, None, "head"),
            P(None, None, "head"),
            P(None, None, "head"),
            P("head", None),
            P("head", None),
            P("head", None),
        ),
        out_specs=(P("ctx", "head"), P("ctx", "head")),
        check_vma=False,
    )
```

time: 168 us -> 130 us (0.77)
  Pallas kernels: 164 us -> 125 us
    pallas_call x2 -> x1, Pallas kernels: 164 us -> 125 us  [fast_body(): pl.pallas_call(functools.partial(block_kernel, ctx_size), out_shape=(jax....]
where the time goes in v1:
time: 130 us
  Pallas kernels  125 us (96%)
  local copies, waits for them, and re-layouts  3.48 us (3%)
    pallas_call x1, Pallas kernels, fast_body(): pl.pallas_call(functools.partial(block_kernel, ctx_size), out_shape=(jax....  125 us
    unnamed x2, local copies, waits for them, and re-layouts  3.48 us

profile of v1, /device:TPU:0, one launch (start us, length us, event | category | flops | bytes accessed | tf_op | source)
XLA Modules:
  0.0 129.6 jit_solution(6793703699948856336)
XLA Ops:
  0.6 125.4 %block.1 = (bf16[768,512]{1,0:T(8,128)(2,1)}, bf16[96,256]{1,0:T(8,128)(2,1)}) custom-call(bf16[768,512]{1,0:T(8,128)(2,1)} %video_ref.1, bf16[96,256]{1,0:T(8,128)(2,1)} %audio_ref.1, f32[1,512]{1,0:T(1,128)} %bitcast.8, f32[1,256]{1,0:T(1,128)} %bitcast.9, bf16[3,4096,512]{2,1,0:T(8,128)(2,1)} %bitcast.5, bf16[3,4096,256]{2,1,0:T(8,128)(2,1)} %bitcast.6, ...), custom_call_target="tpu_custom_call" | custom-call | tf_op jit(solution)/shard_map/block/pallas_call | solution.py:825
  126.1 2.1 %copy.14 = bf16[768,512]{1,0:T(8,128)(2,1)} copy(bf16[768,512]{1,0:T(8,128)(2,1)} %get-tuple-element.4) | data formatting | bytes 1572864
  128.1 1.4 %copy.15 = bf16[96,256]{1,0:T(8,128)(2,1)} copy(bf16[96,256]{1,0:T(8,128)(2,1)} %get-tuple-element.5) | data formatting | bytes 98304

commit v2 on v1

--- a/solution.py
+++ b/solution.py
@@ -258,7 +258,6 @@
     heads,
     sources,
     cross,
-    cross_out,
     tones,
     parts,
     parts_in,
@@ -297,7 +296,6 @@
     me = lax.axis_index("head")
     rows, width = video_ref.shape
     audio_rows, audio_width = audio_ref.shape
-    every_tone = ctx_size * audio_rows
     count = rows // CHUNK
     local_heads = width // HD
     cross_width = w_cross.shape[2]
@@ -338,13 +336,14 @@
         return aligned(block * audio_width, audio_width)
 
     my_tones = aligned(ctx * audio_rows, audio_rows)
-    for k in range(count):
+
+    def scale(k):
         wide = video_ref[pl.ds(k * CHUNK, CHUNK)].astype(F32)
         xs[pl.ds(k * CHUNK, CHUNK), columns(me)] = (wide * video_gain_ref[...]).astype(BF16)
         squares[k : k + 1] = to_row(jnp.sum(wide * wide, axis=1, keepdims=True))
-    every_square[0] = squares[...]
+
+    scale(0)
     raw[my_tones] = audio_ref[...]
-
     pl.semaphore_wait(barrier, len(friends))
 
     def hop(slot, k):
@@ -401,10 +400,13 @@
             (mates[d], me),
         )
 
+    for slot in (6, 2, 4, 1):
+        hop(slot, 0).start()
     for d in others:
         late_copy(0, d).start()
-    for slot in (6, 2, 4, 1):
-        hop(slot, 0).start()
+    for k in range(1, count):
+        scale(k)
+    every_square[0] = squares[...]
     for flip in range(1, 8):
         square_hop(0, flip).start()
 
@@ -450,6 +452,10 @@
 
         lax.fori_loop(0, 3, one, 0)
 
+    def ship(k):
+        for d in others:
+            query_copy(k, d).start()
+
     def project(k, carry):
         at = at_rows(k)
         for slot in (2, 4, 6):
@@ -479,71 +485,71 @@
             return carry
 
         lax.fori_loop(0, 3, one, 0)
+
+        @pl.when(k == count - 2)
+        def _():
+            ship(0)
+
         for plane in range(3):
             sources[ctx, plane, at] = heads[ctx, plane, at]
         return carry
 
     lax.fori_loop(0, count, project, 0)
 
-    def ship(k, carry):
-        for d in others:
-            query_copy(k, d).start()
-        return carry
-
-    lax.fori_loop(0, count, ship, 0)
+    ship(1)
+    ship(2)
     cross_project(count - 1)
 
-    for slot in (2, 4, 6):
-        tone_hop(slot).wait_recv()
-        tone_hop(slot + 1).start()
-    loads[4].wait()
-    for flip in range(1, 8):
-        square_hop(1, flip).wait_recv()
-    for slot in (1, 3, 5, 7):
-        tone_hop(slot).wait_recv()
-    tone_sums = jnp.sum(every_tone_square[...], axis=0)
-    tone_rates = lax.rsqrt(tone_sums / (8 * audio_width) + EPSILON)
-    rate = jnp.concatenate(
-        [to_column(tone_rates[d : d + 1], audio_rows) for d in range(ctx_size)], axis=0
-    )
-    for plane in range(3):
-        acc = jnp.dot(xa[...], w_audio[plane], preferred_element_type=F32)
-        tones[:, plane * cross_width : (plane + 1) * cross_width] = (acc * rate).astype(BF16)
-
-    sound_tile = math.gcd(rows, 256)
+
+    def tone_project():
+        for slot in (2, 4, 6):
+            tone_hop(slot).wait_recv()
+            tone_hop(slot + 1).start()
+        loads[4].wait()
+        for flip in range(1, 8):
+            square_hop(1, flip).wait_recv()
+        for slot in (1, 3, 5, 7):
+            tone_hop(slot).wait_recv()
+        tone_sums = jnp.sum(every_tone_square[...], axis=0)
+        tone_rates = lax.rsqrt(tone_sums / (8 * audio_width) + EPSILON)
+        rate = jnp.concatenate(
+            [to_column(tone_rates[d : d + 1], audio_rows) for d in range(ctx_size)], axis=0
+        )
+        for plane in range(3):
+            acc = jnp.dot(xa[...], w_audio[plane], preferred_element_type=F32)
+            tones[:, plane * cross_width : (plane + 1) * cross_width] = (acc * rate).astype(BF16)
 
     def tone_part_of(plane, h):
         return slice(plane * cross_width + h * HD, plane * cross_width + (h + 1) * HD)
 
-    for h in range(cross_heads):
-        lanes = slice(h * HD, (h + 1) * HD)
-
-        def answer(d, carry):
-            query = tones[aligned(d * audio_rows, audio_rows), tone_part_of(0, h)]
-            mixed, total, highest = softmax_parts(query, [cross[h, 1]], [cross[h, 2]])
-            parts[d, :, lanes] = (mixed / total).astype(BF16)
-            stats[d, 2 * h : 2 * h + 1] = to_row(total)
-            stats[d, 2 * h + 1 : 2 * h + 2] = to_row(highest)
-            return carry
-
-        lax.fori_loop(0, ctx_size, answer, 0)
-    for d in others:
-        late_copy(1, d).start()
-        late_copy(2, d).start()
-    parts_in[ctx] = parts[ctx]
-    stats_in[ctx] = stats[ctx]
-    for h in range(cross_heads):
-        lanes = slice(h * HD, (h + 1) * HD)
-
-        def ask(i, carry):
-            tile = aligned(i * sound_tile, sound_tile)
+    def answer():
+        for h in range(cross_heads):
+            lanes = slice(h * HD, (h + 1) * HD)
+
+            def one(d, carry):
+                query = tones[aligned(d * audio_rows, audio_rows), tone_part_of(0, h)]
+                mixed, total, highest = softmax_parts(query, [cross[h, 1]], [cross[h, 2]])
+                parts[d, :, lanes] = (mixed / total).astype(BF16)
+                stats[d, 2 * h : 2 * h + 1] = to_row(total)
+                stats[d, 2 * h + 1 : 2 * h + 2] = to_row(highest)
+                return carry
+
+            lax.fori_loop(0, ctx_size, one, 0)
+        for d in others:
+            late_copy(1, d).start()
+            late_copy(2, d).start()
+        parts_in[ctx] = parts[ctx]
+        stats_in[ctx] = stats[ctx]
+
+    def ask(k):
+        at = at_rows(k)
+        pieces = []
+        for h in range(cross_heads):
             mixed, total, _ = softmax_parts(
-                cross[h, 0, tile], [tones[:, tone_part_of(1, h)]], [tones[:, tone_part_of(2, h)]]
+                cross[h, 0, at], [tones[:, tone_part_of(1, h)]], [tones[:, tone_part_of(2, h)]]
             )
-            cross_out[tile, lanes] = (mixed / total).astype(BF16)
-            return carry
-
-        lax.fori_loop(0, rows // sound_tile, ask, 0)
+            pieces.append((mixed / total).astype(BF16))
+        return jnp.concatenate(pieces, axis=1)
 
     def settle_hops(k, carry):
         for slot in range(1, 8):
@@ -555,68 +561,52 @@
     lax.fori_loop(0, count, settle_hops, 0)
     for one in loads[5:]:
         one.wait()
-
-    def reducer(part_at, chip, landed, at, side_sems, hop_sems, out_ref, base_ref, parity):
-        near_flip, end_flip = (4, 2) if parity else (2, 4)
-        near, end = near_flip // 2, end_flip // 2
-
+    ones = jnp.ones((rows, HD), BF16)
+    for s in range(ctx_size):
+        w_self[0, s * rows : (s + 1) * rows, :HD] = sources[s, 2]
+        w_self[0, s * rows : (s + 1) * rows, HD : 2 * HD] = ones
+
+    def reducer(part_at, chip, landed, at, side_sems, hop_sems, out_ref, base_ref):
         def side(i):
             return remote(
                 part_at(peer[2 * i + 1]), chip.at[i, at], *side_sems(i), (ctx, peer[1])
             )
 
-        def hop(slot, flip, k):
-            return remote(chip.at[k, at], landed.at[slot, at], *hop_sems(slot), (ctx, peer[flip]))
-
-        def far_hop():
-            return hop(0, near_flip, 3)
-
-        def near_hop():
-            return hop(1, near_flip, near)
-
-        def end_hop():
-            return hop(2, end_flip, end)
+        def hop(i):
+            return remote(
+                chip.at[i, at], landed.at[i - 1, at], *hop_sems(i - 1), (ctx, peer[2 * i])
+            )
 
         def start():
-            for i in (3, near, end, 0):
+            for i in (3, 1, 2, 0):
                 side(i).start()
 
-        def fold(i):
-            side(i).wait_recv()
-            chip[i, at] = (
-                chip[i, at].astype(F32) + part_at(peer[2 * i])[...].astype(F32)
-            ).astype(BF16)
-
         def join():
-            fold(3)
-            far_hop().start()
-            fold(near)
-            near_hop().start()
-            fold(end)
-
-        def pass_on():
-            far_hop().wait_recv()
-            chip[end, at] = (chip[end, at].astype(F32) + landed[0, at].astype(F32)).astype(BF16)
-            end_hop().start()
+            for i in (3, 1, 2):
+                side(i).wait_recv()
+                chip[i, at] = (
+                    chip[i, at].astype(F32) + part_at(peer[2 * i])[...].astype(F32)
+                ).astype(BF16)
+                hop(i).start()
 
         def close():
             side(0).wait_recv()
             total = chip[0, at].astype(F32) + part_at(me)[...].astype(F32)
             total = total + base_ref[at].astype(F32)
-            near_hop().wait_recv()
-            total = total + landed[1, at].astype(F32)
-            end_hop().wait_recv()
-            out_ref[at] = (total + landed[2, at].astype(F32)).astype(BF16)
+            for i in (1, 2, 3):
+                hop(i).wait_recv()
+                total = total + landed[i - 1, at].astype(F32)
+            out_ref[at] = total.astype(BF16)
 
         def settle():
             for i in range(4):
                 side(i).wait_send()
-            for one in (far_hop(), near_hop(), end_hop()):
-                one.wait_send()
-
-        return start, join, pass_on, close, settle
-
-    def video_steps(k, parity):
+            for i in (1, 2, 3):
+                hop(i).wait_send()
+
+        return start, join, close, settle
+
+    def video_steps(k):
         return reducer(
             lambda block: xs.at[at_rows(k), columns(block)],
             chip,
@@ -626,10 +616,9 @@
             lambda slot: (hop_send.at[slot, k], hop_recv.at[slot, k]),
             video_out_ref,
             video_ref,
-            parity,
-        )
-
-    tone_start, tone_join, tone_pass, tone_close, tone_settle = reducer(
+        )
+
+    tone_start, tone_join, tone_close, tone_settle = reducer(
         lambda block: tone_part.at[block],
         tone_chip,
         tone_landed,
@@ -638,7 +627,6 @@
         lambda slot: (tone_out_send.at[4 + slot], tone_out_recv.at[4 + slot]),
         audio_out_ref,
         audio_ref,
-        0,
     )
 
     def sound():
@@ -680,12 +668,22 @@
         at = at_rows(k)
         pair = [mates[(first + i) % ctx_size] for i in range(2)]
         query = jnp.concatenate([sources[s, 0, at] for s in pair], axis=0)
-        mixed, total, _ = softmax_parts(
-            query,
-            [sources[s, 1] for s in range(ctx_size)],
-            [sources[s, 2] for s in range(ctx_size)],
-        )
-        done = (mixed / total).astype(BF16)
+        scores = [contract_last(query, sources[s, 1]) for s in range(ctx_size)]
+        highest = jnp.max(scores[0], axis=1, keepdims=True)
+        mixed = None
+        for s in range(ctx_size):
+            if s:
+                higher = jnp.maximum(highest, jnp.max(scores[s], axis=1, keepdims=True))
+                fade = jnp.exp2((highest - higher) * SCORE_SCALE)
+                highest = higher
+            weight = jnp.exp2((scores[s] - highest) * SCORE_SCALE).astype(BF16)
+            step = jnp.dot(
+                weight,
+                w_self[0, s * rows : (s + 1) * rows, : 2 * HD],
+                preferred_element_type=F32,
+            )
+            mixed = mixed * fade + step if s else step
+        done = (mixed[:, :HD] / mixed[:, HD:]).astype(BF16)
         for i, s in enumerate(pair):
             own[s, at] = done[i * CHUNK : (i + 1) * CHUNK]
             d = (first + i) % ctx_size
@@ -699,80 +697,66 @@
         for d in others:
             back(k, d).wait_recv()
         selfs = jnp.concatenate([mixed_out[s, at] for s in range(ctx_size)], axis=1)
+        crossed = ask(k)
 
         def one(n, carry):
             cols = columns(n)
             xs[at, cols] = (
                 jnp.dot(selfs, w_out[:, cols], preferred_element_type=F32)
-                + jnp.dot(cross_out[at], w_cross_out[:, cols], preferred_element_type=F32)
+                + jnp.dot(crossed, w_cross_out[:, cols], preferred_element_type=F32)
             ).astype(BF16)
             return carry
 
         lax.fori_loop(0, 8, one, 0)
-        video_steps(k, 0)[0]()
-
-    def turn(k, parity):
+        video_steps(k)[0]()
+
+    def turn(k, carry):
         for d in others:
             query_copy(k, d).wait_recv()
         attend_pair(k, 1)
 
+        @pl.when(k >= 3)
+        def _():
+            video_steps(k - 3)[1]()
+
+        attend_pair(k, 3)
+
+        @pl.when(k + 3 < count)
+        def _():
+            ship(k + 3)
+
         @pl.when(k >= 2)
         def _():
-            video_steps(k - 2, parity)[1]()
-
-        attend_pair(k, 3)
-
-        @pl.when(k >= 3)
+            output(k - 2)
+
+        @pl.when(k >= 5)
         def _():
-            video_steps(k - 3, 1 - parity)[2]()
-
-        @pl.when(k >= 1)
-        def _():
-            output(k - 1)
-
-        @pl.when(k >= 4)
-        def _():
-            video_steps(k - 4, parity)[3]()
-
-    def two(i, carry):
-        turn(2 * i, 0)
-
-        @pl.when(i == 1)
-        def _():
-            sound()
-
-        @pl.when(i == 2)
-        def _():
-            tone_pass()
-
-        turn(2 * i + 1, 1)
-
-        @pl.when(i == 1)
-        def _():
-            tone_join()
-
+            video_steps(k - 5)[2]()
+
+        for step, work in ((0, tone_project), (1, answer), (3, sound), (4, tone_join)):
+            pl.when(k == step)(work)
         return carry
 
-    lax.fori_loop(0, count // 2, two, 0)
+    lax.fori_loop(0, count, turn, 0)
     last = count - 1
-    video_steps(last - 1, 0)[1]()
-    video_steps(last - 2, 1)[2]()
+    video_steps(last - 2)[1]()
+    output(last - 1)
+    tone_close()
+    video_steps(last - 4)[2]()
+    video_steps(last - 1)[1]()
     output(last)
-    tone_close()
-    video_steps(last, 1)[1]()
-    video_steps(last - 1, 0)[2]()
-    video_steps(last - 3, 0)[3]()
-    video_steps(last - 2, 1)[3]()
-    video_steps(last, 1)[2]()
-    video_steps(last - 1, 0)[3]()
-    video_steps(last, 1)[3]()
+    video_steps(last - 3)[2]()
+    video_steps(last)[1]()
+    video_steps(last - 2)[2]()
+    video_steps(last - 1)[2]()
+    video_steps(last)[2]()
 
     def finish(k, carry):
         for d in others:
             key_copy(k, d).wait_send()
             query_copy(k, d).wait_send()
             back(k, d).wait_send()
-        video_steps(k, 0)[4]()
+        video_steps(k)[3]()
         return carry
 
     lax.fori_loop(0, count, finish, 0)
@@ -847,7 +831,6 @@
             wide(ctx_size, 3, rows, HD),
             wide(ctx_size, 3, rows, HD),
             wide(cross_heads, 3, rows, HD),
-            wide(rows, cross_width),
             wide(every_tone, 3 * cross_width),
             wide(ctx_size, audio_rows, cross_width),
             wide(ctx_size, audio_rows, cross_width),
@@ -897,13 +880,14 @@
         head_size == 8
         and ctx_size == 4
         and width == ctx_size * HD
-        and rows % (2 * CHUNK) == 0
+        and rows % CHUNK == 0
         and rows >= 6 * CHUNK
         and audio_rows % 16 == 0
         and audio_rows <= HD
         and audio_width % HD == 0
         and video_cross.shape[2] % HD == 0
         and video_cross.shape[2] <= 4 * HD
+        and ctx_size * rows <= video_cross.shape[0]
     )
 
 

time: 130 us -> 125 us (0.962)
  Pallas kernels: 125 us -> 120 us
    pallas_call x1, Pallas kernels: 125 us -> 120 us  [fast_body(): pl.pallas_call(functools.partial(block_kernel, ctx_size), out_shape=(jax....]
where the time goes in v2:
time: 125 us; the launch traced here: 124 us
  Pallas kernels  120 us (96%)
  local copies, waits for them, and re-layouts  3.48 us (3%)
    pallas_call x1, Pallas kernels, fast_body(): pl.pallas_call(functools.partial(block_kernel, ctx_size), out_shape=(jax....  120 us
    unnamed x2, local copies, waits for them, and re-layouts  3.48 us

profile of v2, /device:TPU:0, one launch (start us, length us, event | category | flops | bytes accessed | tf_op | source)
XLA Modules:
  0.0 124.3 jit_solution(15471367462065554402)
XLA Ops:
  0.6 120.2 %block.1 = (bf16[768,512]{1,0:T(8,128)(2,1)}, bf16[96,256]{1,0:T(8,128)(2,1)}) custom-call(bf16[768,512]{1,0:T(8,128)(2,1)} %video_ref.1, bf16[96,256]{1,0:T(8,128)(2,1)} %audio_ref.1, f32[1,512]{1,0:T(1,128)} %bitcast.8, f32[1,256]{1,0:T(1,128)} %bitcast.9, bf16[3,4096,512]{2,1,0:T(8,128)(2,1)} %bitcast.5, bf16[3,4096,256]{2,1,0:T(8,128)(2,1)} %bitcast.6, ...), custom_call_target="tpu_custom_call" | custom-call | tf_op jit(solution)/shard_map/block/pallas_call | solution.py:809
  120.9 2.1 %copy.14 = bf16[768,512]{1,0:T(8,128)(2,1)} copy(bf16[768,512]{1,0:T(8,128)(2,1)} %get-tuple-element.4) | data formatting | bytes 1572864
  122.9 1.4 %copy.15 = bf16[96,256]{1,0:T(8,128)(2,1)} copy(bf16[96,256]{1,0:T(8,128)(2,1)} %get-tuple-element.5) | data formatting | bytes 98304

commit v3 on v2

--- a/solution.py
+++ b/solution.py
@@ -497,7 +497,6 @@
     lax.fori_loop(0, count, project, 0)
 
     ship(1)
-    ship(2)
     cross_project(count - 1)
 
 
@@ -707,7 +706,7 @@
             ).astype(BF16)
             return carry
 
-        lax.fori_loop(0, 8, one, 0)
+        lax.fori_loop(0, 8, one, 0, unroll=2)
         video_steps(k)[0]()
 
     def turn(k, carry):
@@ -715,39 +714,36 @@
             query_copy(k, d).wait_recv()
         attend_pair(k, 1)
 
-        @pl.when(k >= 3)
-        def _():
-            video_steps(k - 3)[1]()
-
-        attend_pair(k, 3)
-
-        @pl.when(k + 3 < count)
-        def _():
-            ship(k + 3)
-
         @pl.when(k >= 2)
         def _():
-            output(k - 2)
-
-        @pl.when(k >= 5)
+            video_steps(k - 2)[1]()
+
+        attend_pair(k, 3)
+
+        @pl.when(k + 2 < count)
         def _():
-            video_steps(k - 5)[2]()
-
-        for step, work in ((0, tone_project), (1, answer), (3, sound), (4, tone_join)):
+            ship(k + 2)
+
+        @pl.when(k >= 1)
+        def _():
+            output(k - 1)
+
+        @pl.when(k >= 4)
+        def _():
+            video_steps(k - 4)[2]()
+
+        for step, work in ((0, tone_project), (3, answer), (4, sound), (5, tone_join)):
             pl.when(k == step)(work)
         return carry
 
     lax.fori_loop(0, count, turn, 0)
     last = count - 1
-    video_steps(last - 2)[1]()
-    output(last - 1)
+    video_steps(last - 1)[1]()
+    video_steps(last - 3)[2]()
+    output(last)
     tone_close()
-    video_steps(last - 4)[2]()
-    video_steps(last - 1)[1]()
-    output(last)
-    video_steps(last - 3)[2]()
+    video_steps(last - 2)[2]()
     video_steps(last)[1]()
-    video_steps(last - 2)[2]()
     video_steps(last - 1)[2]()
     video_steps(last)[2]()
 

time: 125 us -> 121 us (0.968)
  Pallas kernels: 120 us -> 116 us
    pallas_call x1, Pallas kernels: 120 us -> 116 us  [fast_body(): pl.pallas_call(functools.partial(block_kernel, ctx_size), out_shape=(jax....]
where the time goes in v3:
time: 121 us; the launch traced here: 120 us
  Pallas kernels  116 us (96%)
  local copies, waits for them, and re-layouts  3.48 us (3%)
    pallas_call x1, Pallas kernels, fast_body(): pl.pallas_call(functools.partial(block_kernel, ctx_size), out_shape=(jax....  116 us
    unnamed x2, local copies, waits for them, and re-layouts  3.48 us

profile of v3, /device:TPU:0, one launch (start us, length us, event | category | flops | bytes accessed | tf_op | source)
XLA Modules:
  0.0 120.3 jit_solution(18273890317838250430)
XLA Ops:
  0.6 116.1 %block.1 = (bf16[768,512]{1,0:T(8,128)(2,1)}, bf16[96,256]{1,0:T(8,128)(2,1)}) custom-call(bf16[768,512]{1,0:T(8,128)(2,1)} %video_ref.1, bf16[96,256]{1,0:T(8,128)(2,1)} %audio_ref.1, f32[1,512]{1,0:T(1,128)} %bitcast.8, f32[1,256]{1,0:T(1,128)} %bitcast.9, bf16[3,4096,512]{2,1,0:T(8,128)(2,1)} %bitcast.5, bf16[3,4096,256]{2,1,0:T(8,128)(2,1)} %bitcast.6, ...), custom_call_target="tpu_custom_call" | custom-call | tf_op jit(solution)/shard_map/block/pallas_call | solution.py:805
  116.8 2.1 %copy.14 = bf16[768,512]{1,0:T(8,128)(2,1)} copy(bf16[768,512]{1,0:T(8,128)(2,1)} %get-tuple-element.4) | data formatting | bytes 1572864
  118.8 1.4 %copy.15 = bf16[96,256]{1,0:T(8,128)(2,1)} copy(bf16[96,256]{1,0:T(8,128)(2,1)} %get-tuple-element.5) | data formatting | bytes 98304

commit v4 on v3

--- a/solution.py
+++ b/solution.py
@@ -732,7 +732,7 @@
         def _():
             video_steps(k - 4)[2]()
 
-        for step, work in ((0, tone_project), (3, answer), (4, sound), (5, tone_join)):
+        for step, work in ((0, tone_project), (4, answer), (5, sound), (5, tone_join)):
             pl.when(k == step)(work)
         return carry
 

time: 121 us -> 120 us (level)
  no operation moved by 1% of the time
where the time goes in v4:
time: 120 us
  Pallas kernels  116 us (97%)
  local copies, waits for them, and re-layouts  3.48 us (3%)
    pallas_call x1, Pallas kernels, fast_body(): pl.pallas_call(functools.partial(block_kernel, ctx_size), out_shape=(jax....  116 us
    unnamed x2, local copies, waits for them, and re-layouts  3.48 us

profile of v4, /device:TPU:0, one launch (start us, length us, event | category | flops | bytes accessed | tf_op | source)
XLA Modules:
  0.0 120.1 jit_solution(6045922737677435651)
XLA Ops:
  0.6 116.0 %block.1 = (bf16[768,512]{1,0:T(8,128)(2,1)}, bf16[96,256]{1,0:T(8,128)(2,1)}) custom-call(bf16[768,512]{1,0:T(8,128)(2,1)} %video_ref.1, bf16[96,256]{1,0:T(8,128)(2,1)} %audio_ref.1, f32[1,512]{1,0:T(1,128)} %bitcast.8, f32[1,256]{1,0:T(1,128)} %bitcast.9, bf16[3,4096,512]{2,1,0:T(8,128)(2,1)} %bitcast.5, bf16[3,4096,256]{2,1,0:T(8,128)(2,1)} %bitcast.6, ...), custom_call_target="tpu_custom_call" | custom-call | tf_op jit(solution)/shard_map/block/pallas_call | solution.py:805
  116.6 2.1 %copy.14 = bf16[768,512]{1,0:T(8,128)(2,1)} copy(bf16[768,512]{1,0:T(8,128)(2,1)} %get-tuple-element.4) | data formatting | bytes 1572864
  118.7 1.4 %copy.15 = bf16[96,256]{1,0:T(8,128)(2,1)} copy(bf16[96,256]{1,0:T(8,128)(2,1)} %get-tuple-element.5) | data formatting | bytes 98304
